TPU v7x, 512 devices: a whole 4x4x16 slice. The times are simulated.
512 devices in a mesh: dp: 128 (over y_lo, x, z), mp: 4 (over y_hi, core).
Axes of the slice: x: 4, y: 4 (y_hi: 2, y_lo: 2; y = y_hi * 2 + y_lo), z: 16, core: 2. Of those that a mesh axis runs over, the one named last changes fastest.
Arguments:
- vlm_tokens: bfloat16 [32768, 2048], P(('dp', 'mp')), may hold values from -64 to 64
- action_tokens: bfloat16 [65536, 2048], P(('dp', 'mp')), may hold values from -64 to 64
- norm_gain: float32 [2048], replicated, may hold values from 0.25 to 1.75
- proj_old: bfloat16 [4096, 4096], P('dp', 'mp'), may hold values from -0.125 to 0.125
Outputs:
- vlm_hidden: bfloat16 [65536, 4096], P('dp', 'mp')
- action_hidden: bfloat16 [65536, 8192], P('dp', 'mp')
- proj_new: bfloat16 [2048, 8192], P('dp', 'mp')
All inputs are finite; a program needn't handle non-finite values.
Results may differ from a plain program's by a relative error of at most 0.005.
Values may be sent and summed in bfloat16 or wider, within the bound.
No kernel may reach another device: no remote copies, remote signals or barrier semaphores. Data moves between devices by JAX's collectives and lax.ppermute only.
A program may use at most 64 MiB of HBM per device.

v0:
```python
import jax
import jax.numpy as jnp
from jax import lax
from jax.experimental import pallas as pl
from jax.experimental.pallas import tpu as pltpu
from jax.sharding import Mesh
from jax.sharding import PartitionSpec as P


ALL = ("y", "x", "u", "w", "h", "c")
NX, NU, NW = 4, 4, 4
PLANE = ("x", "u", "w", "c")

epsilon = 1e-06


def normalize(row_values, norm_gain):
    values = row_values.astype(jnp.float32)
    factor = lax.rsqrt(jnp.mean(values * values, axis=-1, keepdims=True) + epsilon)
    return (values * factor * norm_gain).astype(jnp.bfloat16)


def swap(array, axis):
    return lax.ppermute(array, axis, [(0, 1), (1, 0)])


def swap_parity(array):
    return lax.ppermute(array, "w", [(i, i ^ 1) for i in range(NW)])


def along(array, x_core, ahead):
    pairs = []
    for x in range(NX):
        for z in range(NU * NW):
            for c in range(2):
                sx, sz = ((x + ahead) % NX, z) if c == x_core else (x, (z + ahead) % (NU * NW))
                pairs.append(((sx * NU * NW + sz) * 2 + c, (x * NU * NW + z) * 2 + c))
    return lax.ppermute(array, PLANE, pairs)


def both(flag, own, other, dim):
    first = jnp.where(flag == 0, own, other)
    second = jnp.where(flag == 0, other, own)
    return jnp.concatenate([first, second], dim)


def in_place(parts, me):
    n = len(parts)
    twice = jnp.stack(parts + parts[:-1])
    return lax.dynamic_slice_in_dim(twice, (n - me) % n, n, 0)


def near_weight(proj_old):
    y, x, w, c = (lax.axis_index(a) for a in "yxwc")
    half = proj_old.shape[1] // 2
    mine = lax.dynamic_slice_in_dim(proj_old, c * half, half, 1)
    given = lax.dynamic_slice_in_dim(proj_old, (1 - c) * half, half, 1)
    piece = both(c, mine[None], swap(given, "c")[None], 0)
    far = [piece] + [lax.ppermute(piece, "u", [((i + d) % NU, i) for i in range(NU)]) for d in (2, 1, 3)]
    far[1], far[2] = far[2], far[1]
    mates = in_place(far, lax.axis_index("u"))
    other = swap(mates, "y")
    planes = both(y, mates[None], other[None], 0)
    near = [planes] + [along(planes, 1, d) for d in (1, 2, -1)]
    return in_place(near, jnp.where(c == 0, w, x))


def all_weight(slab):
    low, high = slab[: slab.shape[0] // 2], slab[slab.shape[0] // 2 :]
    low_prev = along(low, 0, -1)
    high_next = along(high, 0, 1)
    high_prev = along(high, 0, -1)
    low_next = along(low, 0, 1)
    low_far = along(low_prev, 0, -1)
    high_far = along(high_next, 0, 1)
    return (low, high, low_next, high_next, low_far, high_far, low_prev, high_prev)


def chip_tokens(vlm_tokens, action_tokens, norm_gain):
    vlm = normalize(vlm_tokens, norm_gain)
    action = normalize(action_tokens, norm_gain)
    other = swap_parity(vlm)
    pair = both(lax.axis_index("w") % 2, vlm, other, 0)
    return jnp.concatenate([pair, action], 0)


def all_tokens(mine, n_vlm):
    h, c = lax.axis_index("h"), lax.axis_index("c")
    width = mine.shape[1]
    other = swap(mine, "h")
    two = both(h, mine[None], other[None], 0)
    theirs = swap(two, "c")
    four = jnp.stack([jnp.where(c == 0, two, theirs), jnp.where(c == 0, theirs, two)], 1)
    four = four.reshape(4, -1, width)
    normed_vlm = four[:, : 2 * n_vlm].reshape(4, 2, n_vlm, width).transpose(1, 0, 2, 3).reshape(-1, width)
    return normed_vlm, four[:, 2 * n_vlm :].reshape(-1, width)


def new_projection(proj_old):
    b = lax.axis_index("w") % 2
    row_half = proj_old.shape[0] // 2
    kept = lax.dynamic_slice_in_dim(proj_old, b * row_half, row_half, 0)
    given = lax.dynamic_slice_in_dim(proj_old, (1 - b) * row_half, row_half, 0)
    return both(b, kept, swap_parity(given), 1)


def gelu(total):
    return total * 0.5 * (1.0 + lax.erf(total * 0.7071067811865476))


ROWS = 256


def products(place, core, vlm, action, slabs, weight, sems, store):
    x, w, c = (place[i] for i in range(3))
    copies = []
    for r in range(4):
        for s in range(2):
            ref = slabs[2 * r + s]
            for t in range(2):
                q = 2 * s + t
                col = jnp.where(c == 0, lax.rem(x + r, 4), q)
                row = jnp.where(c == 0, q, lax.rem(w + r, 4))
                for y in range(2):
                    copies.append(
                        pltpu.make_async_copy(
                            ref.at[t, y, :, core],
                            weight.at[lax.rem(row, 2), y, col, :, row // 2],
                            sems.at[len(copies)],
                        )
                    )
    for copy in copies:
        copy.start()
    for copy in copies:
        copy.wait()
    depth, half = action.shape[1], weight.shape[-1]
    for block in range(3):
        rows, parity = (action, block) if block < 2 else (vlm, lax.rem(w, 2))
        columns = weight[parity].reshape(depth, half)
        for i in range(0, rows.shape[0], ROWS):
            total = jnp.dot(rows[i : i + ROWS, :], columns, preferred_element_type=jnp.float32)
            store(block, i, gelu(total).astype(jnp.bfloat16))


def given_kernel(place, vlm, action, *refs):
    slabs, (out, weight, sems) = refs[:8], refs[8:]

    def store(block, i, values):
        out[block, i : i + ROWS, :] = values

    products(place, 1 - place[2], vlm, action, slabs, weight, sems, store)


def column_copies(core, parts, vlm_out, action_out, sems):
    half = parts.shape[-1]
    b_copies = [
        pltpu.make_async_copy(
            parts.at[b], action_out.at[:, pl.ds(pl.multiple_of((2 * b + core) * half, half), half)], sems.at[b]
        )
        for b in range(2)
    ]
    vlm_copy = pltpu.make_async_copy(
        parts.at[2], vlm_out.at[:, pl.ds(pl.multiple_of(core * half, half), half)], sems.at[2]
    )
    return b_copies + [vlm_copy]


def own_kernel(place, vlm, action, *refs):
    slabs, (vlm_out, action_out, weight, stage, sems, out_sems) = refs[:8], refs[8:]
    outs = column_copies(place[2], stage, vlm_out, action_out, out_sems)

    def store(block, i, values):
        stage[block, i : i + ROWS, :] = values
        if i + ROWS == stage.shape[1]:
            outs[block].start()

    products(place, place[2], vlm, action, slabs, weight, sems, store)
    for copy in outs:
        copy.wait()


def merge_kernel(place, parts, vlm_in, action_in, vlm_out, action_out, sems):
    del vlm_in, action_in
    copies = column_copies(1 - place[2], parts, vlm_out, action_out, sems)
    for copy in copies:
        copy.start()
    for copy in copies:
        copy.wait()


SMEM = pl.BlockSpec(memory_space=pltpu.SMEM)
VMEM = pl.BlockSpec(memory_space=pltpu.VMEM)
HBM = pl.BlockSpec(memory_space=pltpu.HBM)


def outputs(vlm, action, slabs):
    place = jnp.stack([lax.axis_index(a) for a in "xwc"]).astype(jnp.int32)
    half, rows, count = slabs[0].shape[-1], slabs[0].shape[-2], action.shape[0]
    cost = pl.CostEstimate(
        flops=6 * count * action.shape[1] * half, bytes_accessed=12 * 1024 * 1024, transcendentals=0
    )
    params = pltpu.CompilerParams(vmem_limit_bytes=20 * 1024 * 1024)
    weight = pltpu.VMEM((2, 2, NX, NU, 2, rows, half), jnp.bfloat16)
    sems = pltpu.SemaphoreType.DMA((32,))
    parts = jax.ShapeDtypeStruct((3, count, half), jnp.bfloat16)
    wide = (
        jax.ShapeDtypeStruct((count, 2 * half), jnp.bfloat16),
        jax.ShapeDtypeStruct((count, 4 * half), jnp.bfloat16),
    )
    given = pl.pallas_call(
        given_kernel,
        out_shape=parts,
        in_specs=[SMEM, VMEM, VMEM] + [HBM] * 8,
        out_specs=VMEM,
        scratch_shapes=[weight, sems],
        compiler_params=params,
        cost_estimate=cost,
        name="given",
    )(place, vlm, action, *slabs)
    own = pl.pallas_call(
        own_kernel,
        out_shape=wide,
        in_specs=[SMEM, VMEM, VMEM] + [HBM] * 8,
        out_specs=(HBM, HBM),
        scratch_shapes=[weight, pltpu.VMEM(parts.shape, parts.dtype), sems, pltpu.SemaphoreType.DMA((3,))],
        compiler_params=params,
        cost_estimate=cost,
        name="own",
    )(place, vlm, action, *slabs)
    taken = swap(given, "c")
    return pl.pallas_call(
        merge_kernel,
        out_shape=wide,
        in_specs=[SMEM, HBM, HBM, HBM],
        out_specs=(HBM, HBM),
        scratch_shapes=[pltpu.SemaphoreType.DMA((3,))],
        input_output_aliases={2: 0, 3: 1},
        name="merge",
    )(place, taken, *own)


def local(vlm_tokens, action_tokens, norm_gain, proj_old):
    slab, mine = near_weight(proj_old), chip_tokens(vlm_tokens, action_tokens, norm_gain)
    slab, mine = lax.optimization_barrier((slab, mine))
    slabs = all_weight(slab)
    vlm, action = all_tokens(mine, vlm_tokens.shape[0])
    vlm_hidden, action_hidden = outputs(vlm, action, slabs)
    return (vlm_hidden, action_hidden, new_projection(proj_old))


def solution(mesh):
    finer = Mesh(mesh.devices.reshape(2, NX, NU, NW, 2, 2), ALL)
    dp, mp = ALL[:4], ALL[4:]
    in_specs = (P(ALL, None), P(ALL, None), P(), P(dp, mp))
    out_specs = (P(dp, mp), P(dp, mp), P(dp, mp))
    return jax.shard_map(local, mesh=finer, in_specs=in_specs, out_specs=out_specs, check_vma=False)
```

profile of v0, /device:TPU:1, one launch (start us, length us, event | category | flops | bytes accessed | tf_op | source)
XLA Modules:
  0.0 230.4 jit_solution(6692073242987084059)
XLA Ops:
  1.5 8.7 %collective-permute-start = (bf16[32,512]{1,0:T(8,128)(2,1)S(1)}, bf16[32,512]{1,0:T(8,128)(2,1)S(1)}, u32[]{:S(2)}, u32[]{:S(2)}) collective-permute-start(bf16[32,512]{1,0:T(8,128)(2,1)S(1)} %constant_dynamic-slice_fusion.3), channel_id=1, source_target_pairs={{0,1},{1,0},{2,3},{3,2},{4,5},{5,4},{6,7},{7,6},{8,9},{9,8},{10,11... | collective-permute-start | bytes 98312 | tf_op jit(solution)/shard_map/ppermute | solution.py:24
  16.5 7.8 %collective-permute-start.1 = (bf16[2,32,512]{2,1,0:T(8,128)(2,1)S(1)}, bf16[2,32,512]{2,1,0:T(8,128)(2,1)S(1)}, u32[]{:S(2)}, u32[]{:S(2)}) collective-permute-start(bf16[2,32,512]{2,1,0:T(8,128)(2,1)S(1)} %pad_maximum_fusion.4), channel_id=1, source_target_pairs={{16,0},{32,16},{48,32},{0,48},{17,1},{33,17},{49,33},{1,49},{18,2}... | collective-permute-start | bytes 196616 | tf_op jit(solution)/shard_map/ppermute | solution.py:59
  24.3 4.9 %collective-permute-start.2 = (bf16[2,32,512]{2,1,0:T(8,128)(2,1)S(1)}, bf16[2,32,512]{2,1,0:T(8,128)(2,1)S(1)}, u32[]{:S(2)}, u32[]{:S(2)}) collective-permute-start(bf16[2,32,512]{2,1,0:T(8,128)(2,1)S(1)} %pad_maximum_fusion.4), channel_id=1, source_target_pairs={{32,0},{48,16},{0,32},{16,48},{33,1},{49,17},{1,33},{17,49},{34,2}... | collective-permute-start | bytes 196616 | tf_op jit(solution)/shard_map/ppermute | solution.py:59
  29.2 7.3 %collective-permute-start.3 = (bf16[2,32,512]{2,1,0:T(8,128)(2,1)S(1)}, bf16[2,32,512]{2,1,0:T(8,128)(2,1)S(1)}, u32[]{:S(2)}, u32[]{:S(2)}) collective-permute-start(bf16[2,32,512]{2,1,0:T(8,128)(2,1)S(1)} %pad_maximum_fusion.4), channel_id=1, source_target_pairs={{48,0},{0,16},{16,32},{32,48},{49,1},{1,17},{17,33},{33,49},{50,2}... | collective-permute-start | bytes 196616 | tf_op jit(solution)/shard_map/ppermute | solution.py:59
  38.3 4.1 %collective-permute-done.3 = bf16[2,32,512]{2,1,0:T(8,128)(2,1)S(1)} collective-permute-done((bf16[2,32,512]{2,1,0:T(8,128)(2,1)S(1)}, bf16[2,32,512]{2,1,0:T(8,128)(2,1)S(1)}, u32[]{:S(2)}, u32[]{:S(2)}) %collective-permute-start.3) | collective-permute-done | bytes 65568 | tf_op jit(solution)/shard_map/ppermute | solution.py:59
  42.5 2.7 %collective-permute-start.4 = (bf16[4,2,32,512]{3,2,1,0:T(8,128)(2,1)S(1)}, bf16[4,2,32,512]{3,2,1,0:T(8,128)(2,1)S(1)}, u32[]{:S(2)}, u32[]{:S(2)}) collective-permute-start(bf16[4,2,32,512]{3,2,1,0:T(8,128)(2,1)S(1)} %constant_dynamic-slice_fusion.2), channel_id=1, source_target_pairs={{0,256},{256,0},{1,257},{257,1},{2,258},{258,2},{3,259},{259,3},{4... | collective-permute-start | bytes 786440 | tf_op jit(solution)/shard_map/ppermute | solution.py:24
  45.4 6.4 %collective-permute-done.4 = bf16[4,2,32,512]{3,2,1,0:T(8,128)(2,1)S(1)} collective-permute-done((bf16[4,2,32,512]{3,2,1,0:T(8,128)(2,1)S(1)}, bf16[4,2,32,512]{3,2,1,0:T(8,128)(2,1)S(1)}, u32[]{:S(2)}, u32[]{:S(2)}) %collective-permute-start.4) | collective-permute-done | bytes 262176 | tf_op jit(solution)/shard_map/ppermute | solution.py:24
  51.9 3.8 %collective-permute-start.5 = (bf16[2,4,2,32,512]{4,3,2,1,0:T(8,128)(2,1)S(1)}, bf16[2,4,2,32,512]{4,3,2,1,0:T(8,128)(2,1)S(1)}, u32[]{:S(2)}, u32[]{:S(2)}) collective-permute-start(bf16[2,4,2,32,512]{4,3,2,1,0:T(8,128)(2,1)S(1)} %pad_maximum_fusion.3), channel_id=1, source_target_pairs={{4,0},{65,1},{8,4},{69,5},{12,8},{73,9},{16,12},{77,13},{20,16},{8... | collective-permute-start | bytes 1572872 | tf_op jit(solution)/shard_map/ppermute | solution.py:38
  61.1 6.4 %collective-permute-done.5 = bf16[2,4,2,32,512]{4,3,2,1,0:T(8,128)(2,1)S(1)} collective-permute-done((bf16[2,4,2,32,512]{4,3,2,1,0:T(8,128)(2,1)S(1)}, bf16[2,4,2,32,512]{4,3,2,1,0:T(8,128)(2,1)S(1)}, u32[]{:S(2)}, u32[]{:S(2)}) %collective-permute-start.5) | collective-permute-done | bytes 524320 | tf_op jit(solution)/shard_map/ppermute | solution.py:38
  67.6 5.8 %collective-permute-done.7 = bf16[2,4,2,32,512]{4,3,2,1,0:T(8,128)(2,1)S(1)} collective-permute-done((bf16[2,4,2,32,512]{4,3,2,1,0:T(8,128)(2,1)S(1)}, bf16[2,4,2,32,512]{4,3,2,1,0:T(8,128)(2,1)S(1)}, u32[]{:S(2)}, u32[]{:S(2)}) %collective-permute-start.7) | collective-permute-done | bytes 524320 | tf_op jit(solution)/shard_map/ppermute | solution.py:38
  73.8 4.8 %collective-permute-start.9 = (bf16[256,2048]{1,0:T(8,128)(2,1)S(1)}, bf16[256,2048]{1,0:T(8,128)(2,1)}, u32[]{:S(2)}, u32[]{:S(2)}) collective-permute-start(bf16[256,2048]{1,0:T(8,128)(2,1)S(1)} %pad_maximum_fusion.2), channel_id=1, source_target_pairs={{0,2},{2,0},{1,3},{3,1},{4,6},{6,4},{5,7},{7,5},{8,10},{10,8},{9,1... | collective-permute-start | bytes 3145736 | tf_op jit(solution)/shard_map/ppermute | solution.py:24
  78.6 17.4 %collective-permute-done.9 = bf16[256,2048]{1,0:T(8,128)(2,1)} collective-permute-done((bf16[256,2048]{1,0:T(8,128)(2,1)S(1)}, bf16[256,2048]{1,0:T(8,128)(2,1)}, u32[]{:S(2)}, u32[]{:S(2)}) %collective-permute-start.9) | collective-permute-done | bytes 1048608 | tf_op jit(solution)/shard_map/ppermute | solution.py:24
  97.6 8.7 %collective-permute-start.10 = (bf16[2,256,2048]{2,1,0:T(8,128)(2,1)S(1)}, bf16[2,256,2048]{2,1,0:T(8,128)(2,1)S(1)}, u32[]{:S(2)}, u32[]{:S(2)}) collective-permute-start(bf16[2,256,2048]{2,1,0:T(8,128)(2,1)S(1)} %pad_maximum_fusion.1), channel_id=1, source_target_pairs={{0,1},{1,0},{2,3},{3,2},{4,5},{5,4},{6,7},{7,6},{8,9},{9,8},{10,11... | collective-permute-start | bytes 6291464 | tf_op jit(solution)/shard_map/ppermute | solution.py:24
  106.5 4.1 %collective-permute-start.13 = (bf16[2,2,4,2,32,512]{5,4,3,2,1,0:T(8,128)(2,1)S(1)}, bf16[2,2,4,2,32,512]{5,4,3,2,1,0:T(8,128)(2,1)S(1)}, u32[]{:S(2)}, u32[]{:S(2)}) collective-permute-start(bf16[2,2,4,2,32,512]{5,4,3,2,1,0:T(8,128)(2,1)S(1)} %get-tuple-element.20.refs_0_), channel_id=1, source_target_pairs={{192,0},{61,1},{196,4},{1,5},{200,8},{5,9},{204,12},{9,13},{208,16... | collective-permute-start | bytes 3145736 | tf_op jit(solution)/shard_map/ppermute | solution.py:38
  110.6 3.4 %collective-permute-start.12 = (bf16[2,2,4,2,32,512]{5,4,3,2,1,0:T(8,128)(2,1)S(1)}, bf16[2,2,4,2,32,512]{5,4,3,2,1,0:T(8,128)(2,1)S(1)}, u32[]{:S(2)}, u32[]{:S(2)}) collective-permute-start(bf16[2,2,4,2,32,512]{5,4,3,2,1,0:T(8,128)(2,1)S(1)} %get-tuple-element.19.refs_1_), channel_id=1, source_target_pairs={{64,0},{5,1},{68,4},{9,5},{72,8},{13,9},{76,12},{17,13},{80,16},{2... | collective-permute-start | bytes 3145736 | tf_op jit(solution)/shard_map/ppermute | solution.py:38
  114.1 3.4 %collective-permute-start.11 = (bf16[2,2,4,2,32,512]{5,4,3,2,1,0:T(8,128)(2,1)S(1)}, bf16[2,2,4,2,32,512]{5,4,3,2,1,0:T(8,128)(2,1)S(1)}, u32[]{:S(2)}, u32[]{:S(2)}) collective-permute-start(bf16[2,2,4,2,32,512]{5,4,3,2,1,0:T(8,128)(2,1)S(1)} %get-tuple-element.20.refs_0_), channel_id=1, source_target_pairs={{64,0},{5,1},{68,4},{9,5},{72,8},{13,9},{76,12},{17,13},{80,16},{2... | collective-permute-start | bytes 3145736 | tf_op jit(solution)/shard_map/ppermute | solution.py:38
  119.4 5.2 %collective-permute-done.13.refs_6_ = bf16[2,2,4,2,32,512]{5,4,3,2,1,0:T(8,128)(2,1)S(1)} collective-permute-done((bf16[2,2,4,2,32,512]{5,4,3,2,1,0:T(8,128)(2,1)S(1)}, bf16[2,2,4,2,32,512]{5,4,3,2,1,0:T(8,128)(2,1)S(1)}, u32[]{:S(2)}, u32[]{:S(2)}) %collective-permute-start.13) | collective-permute-done | bytes 1048608 | tf_op jit(solution)/shard_map/ppermute | solution.py:38
  126.5 4.6 %collective-permute-start.15 = (bf16[2,2,4,2,32,512]{5,4,3,2,1,0:T(8,128)(2,1)S(1)}, bf16[2,2,4,2,32,512]{5,4,3,2,1,0:T(8,128)(2,1)S(1)}, u32[]{:S(2)}, u32[]{:S(2)}) collective-permute-start(bf16[2,2,4,2,32,512]{5,4,3,2,1,0:T(8,128)(2,1)S(1)} %collective-permute-done.12.refs_3_), channel_id=1, source_target_pairs={{64,0},{5,1},{68,4},{9,5},{72,8},{13,9},{76,12},{17,13},{80,16},{2... | collective-permute-start | bytes 3145736 | tf_op jit(solution)/shard_map/ppermute | solution.py:38
  132.4 5.4 %collective-permute-done.11.refs_2_ = bf16[2,2,4,2,32,512]{5,4,3,2,1,0:T(8,128)(2,1)S(1)} collective-permute-done((bf16[2,2,4,2,32,512]{5,4,3,2,1,0:T(8,128)(2,1)S(1)}, bf16[2,2,4,2,32,512]{5,4,3,2,1,0:T(8,128)(2,1)S(1)}, u32[]{:S(2)}, u32[]{:S(2)}) %collective-permute-start.11) | collective-permute-done | bytes 1048608 | tf_op jit(solution)/shard_map/ppermute | solution.py:38
  137.7 9.0 %collective-permute-done.14.refs_4_ = bf16[2,2,4,2,32,512]{5,4,3,2,1,0:T(8,128)(2,1)S(1)} collective-permute-done((bf16[2,2,4,2,32,512]{5,4,3,2,1,0:T(8,128)(2,1)S(1)}, bf16[2,2,4,2,32,512]{5,4,3,2,1,0:T(8,128)(2,1)S(1)}, u32[]{:S(2)}, u32[]{:S(2)}) %collective-permute-start.14) | collective-permute-done | bytes 1048608 | tf_op jit(solution)/shard_map/ppermute | solution.py:38
  148.7 7.4 %given.1 = bf16[3,512,512]{2,1,0:T(8,128)(2,1)} custom-call(s32[3]{0:T(128)S(1)} %pad_add_fusion.place, bf16[512,2048]{1,0:T(8,128)(2,1)S(1)} %bitcast.49, bf16[512,2048]{1,0:T(8,128)(2,1)S(1)} %bitcast.51, bf16[2,2,4,2,32,512]{5,4,3,2,1,0:T(8,128)(2,1)S(1)} %get-tuple-element.20.refs_0_, bf16[2,2,4,2,32,512]{5,4,3,2,1,0:T(8,128)(2,1)S(1)} %get-tuple-element.19.refs_1_, ...), custom_call_target="tpu_custom_call" | custom-call | flops 3221225472 | bytes 12582912 | tf_op jit(solution)/shard_map/given/pallas_call | solution.py:210
  158.1 3.8 %collective-permute-start.18 = (bf16[16,1024]{1,0:T(8,128)(2,1)S(1)}, bf16[16,1024]{1,0:T(8,128)(2,1)S(1)}, u32[]{:S(2)}, u32[]{:S(2)}) collective-permute-start(bf16[16,1024]{1,0:T(8,128)(2,1)S(1)} %constant_dynamic-slice_fusion), channel_id=1, source_target_pairs={{0,4},{4,0},{8,12},{12,8},{1,5},{5,1},{9,13},{13,9},{2,6},{6,2},{1... | collective-permute-start | bytes 98312 | tf_op jit(solution)/shard_map/ppermute | solution.py:28
  174.0 7.0 %own.1 = (bf16[512,1024]{1,0:T(8,128)(2,1)}, bf16[512,2048]{1,0:T(8,128)(2,1)}) custom-call(s32[3]{0:T(128)S(1)} %pad_add_fusion.place, bf16[512,2048]{1,0:T(8,128)(2,1)S(1)} %bitcast.50, bf16[512,2048]{1,0:T(8,128)(2,1)S(1)} %bitcast.52, bf16[2,2,4,2,32,512]{5,4,3,2,1,0:T(8,128)(2,1)S(1)} %copy-done.3, ...), custom_call_target="tpu_custom_call" | custom-call | flops 3221225472 | bytes 12582912 | tf_op jit(solution)/shard_map/own/pallas_call | solution.py:220
  181.0 49.4 %merge.1 = (bf16[512,1024]{1,0:T(8,128)(2,1)}, bf16[512,2048]{1,0:T(8,128)(2,1)}) custom-call(s32[3]{0:T(128)} %copy-done.16, bf16[3,512,512]{2,1,0:T(8,128)(2,1)} %collective-permute-done.17.parts, bf16[512,1024]{1,0:T(8,128)(2,1)} %get-tuple-element.11.vlm_in, ...), custom_call_target="tpu_custom_call", output_to_operand_aliasing={{0}: (2, {}), {1}: (3, {})} | custom-call | tf_op jit(solution)/shard_map/merge/pallas_call | solution.py:231
  (99 shorter events, 37.7 us)
Async XLA Ops:
  0.6 44.6 %copy-start.20 = (f32[2048]{0:T(1024)S(1)}, f32[2048]{0:T(1024)}, u32[]{:S(2)}) copy-start(f32[2048]{0:T(1024)} %param.6) | copy-start | bytes 24580
  0.6 44.6 %copy-start.18 = (bf16[128,2048]{1,0:T(8,128)(2,1)S(1)}, bf16[128,2048]{1,0:T(8,128)(2,1)}, u32[]{:S(2)}) copy-start(bf16[128,2048]{1,0:T(8,128)(2,1)} %param.5) | copy-start | bytes 1572868
  1.5 14.2 %collective-permute-start = (bf16[32,512]{1,0:T(8,128)(2,1)S(1)}, bf16[32,512]{1,0:T(8,128)(2,1)S(1)}, u32[]{:S(2)}, u32[]{:S(2)}) collective-permute-start(bf16[32,512]{1,0:T(8,128)(2,1)S(1)} %constant_dynamic-slice_fusion.3), channel_id=1, source_target_pairs={{0,1},{1,0},{2,3},{3,2},{4,5},{5,4},{6,7},{7,6},{8,9},{9,8},{10,11... | collective-permute-start | bytes 98312 | tf_op jit(solution)/shard_map/ppermute | solution.py:24
  12.4 43.3 %collective-permute-start.8 = (bf16[64,2048]{1,0:T(8,128)(2,1)S(1)}, bf16[64,2048]{1,0:T(8,128)(2,1)S(1)}, u32[]{:S(2)}, u32[]{:S(2)}) collective-permute-start(bf16[64,2048]{1,0:T(8,128)(2,1)S(1)} %fusion.5), channel_id=1, source_target_pairs={{0,4},{4,0},{8,12},{12,8},{1,5},{5,1},{9,13},{13,9},{2,6},{6,2},{1... | collective-permute-start | bytes 786440 | tf_op jit(solution)/shard_map/ppermute | solution.py:28
  16.5 20.1 %collective-permute-start.1 = (bf16[2,32,512]{2,1,0:T(8,128)(2,1)S(1)}, bf16[2,32,512]{2,1,0:T(8,128)(2,1)S(1)}, u32[]{:S(2)}, u32[]{:S(2)}) collective-permute-start(bf16[2,32,512]{2,1,0:T(8,128)(2,1)S(1)} %pad_maximum_fusion.4), channel_id=1, source_target_pairs={{16,0},{32,16},{48,32},{0,48},{17,1},{33,17},{49,33},{1,49},{18,2}... | collective-permute-start | bytes 196616 | tf_op jit(solution)/shard_map/ppermute | solution.py:59
  24.3 14.0 %collective-permute-start.2 = (bf16[2,32,512]{2,1,0:T(8,128)(2,1)S(1)}, bf16[2,32,512]{2,1,0:T(8,128)(2,1)S(1)}, u32[]{:S(2)}, u32[]{:S(2)}) collective-permute-start(bf16[2,32,512]{2,1,0:T(8,128)(2,1)S(1)} %pad_maximum_fusion.4), channel_id=1, source_target_pairs={{32,0},{48,16},{0,32},{16,48},{33,1},{49,17},{1,33},{17,49},{34,2}... | collective-permute-start | bytes 196616 | tf_op jit(solution)/shard_map/ppermute | solution.py:59
  29.2 13.2 %collective-permute-start.3 = (bf16[2,32,512]{2,1,0:T(8,128)(2,1)S(1)}, bf16[2,32,512]{2,1,0:T(8,128)(2,1)S(1)}, u32[]{:S(2)}, u32[]{:S(2)}) collective-permute-start(bf16[2,32,512]{2,1,0:T(8,128)(2,1)S(1)} %pad_maximum_fusion.4), channel_id=1, source_target_pairs={{48,0},{0,16},{16,32},{32,48},{49,1},{1,17},{17,33},{33,49},{50,2}... | collective-permute-start | bytes 196616 | tf_op jit(solution)/shard_map/ppermute | solution.py:59
  42.5 9.3 %collective-permute-start.4 = (bf16[4,2,32,512]{3,2,1,0:T(8,128)(2,1)S(1)}, bf16[4,2,32,512]{3,2,1,0:T(8,128)(2,1)S(1)}, u32[]{:S(2)}, u32[]{:S(2)}) collective-permute-start(bf16[4,2,32,512]{3,2,1,0:T(8,128)(2,1)S(1)} %constant_dynamic-slice_fusion.2), channel_id=1, source_target_pairs={{0,256},{256,0},{1,257},{257,1},{2,258},{258,2},{3,259},{259,3},{4... | collective-permute-start | bytes 786440 | tf_op jit(solution)/shard_map/ppermute | solution.py:24
  51.9 15.6 %collective-permute-start.5 = (bf16[2,4,2,32,512]{4,3,2,1,0:T(8,128)(2,1)S(1)}, bf16[2,4,2,32,512]{4,3,2,1,0:T(8,128)(2,1)S(1)}, u32[]{:S(2)}, u32[]{:S(2)}) collective-permute-start(bf16[2,4,2,32,512]{4,3,2,1,0:T(8,128)(2,1)S(1)} %pad_maximum_fusion.3), channel_id=1, source_target_pairs={{4,0},{65,1},{8,4},{69,5},{12,8},{73,9},{16,12},{77,13},{20,16},{8... | collective-permute-start | bytes 1572872 | tf_op jit(solution)/shard_map/ppermute | solution.py:38
  56.0 11.5 %collective-permute-start.6 = (bf16[2,4,2,32,512]{4,3,2,1,0:T(8,128)(2,1)S(1)}, bf16[2,4,2,32,512]{4,3,2,1,0:T(8,128)(2,1)S(1)}, u32[]{:S(2)}, u32[]{:S(2)}) collective-permute-start(bf16[2,4,2,32,512]{4,3,2,1,0:T(8,128)(2,1)S(1)} %pad_maximum_fusion.3), channel_id=1, source_target_pairs={{8,0},{129,1},{12,4},{133,5},{16,8},{137,9},{20,12},{141,13},{24,1... | collective-permute-start | bytes 1572872 | tf_op jit(solution)/shard_map/ppermute | solution.py:38
  58.5 14.8 %collective-permute-start.7 = (bf16[2,4,2,32,512]{4,3,2,1,0:T(8,128)(2,1)S(1)}, bf16[2,4,2,32,512]{4,3,2,1,0:T(8,128)(2,1)S(1)}, u32[]{:S(2)}, u32[]{:S(2)}) collective-permute-start(bf16[2,4,2,32,512]{4,3,2,1,0:T(8,128)(2,1)S(1)} %pad_maximum_fusion.3), channel_id=1, source_target_pairs={{60,0},{193,1},{0,4},{197,5},{4,8},{201,9},{8,12},{205,13},{12,16}... | collective-permute-start | bytes 1572872 | tf_op jit(solution)/shard_map/ppermute | solution.py:38
  73.8 22.2 %collective-permute-start.9 = (bf16[256,2048]{1,0:T(8,128)(2,1)S(1)}, bf16[256,2048]{1,0:T(8,128)(2,1)}, u32[]{:S(2)}, u32[]{:S(2)}) collective-permute-start(bf16[256,2048]{1,0:T(8,128)(2,1)S(1)} %pad_maximum_fusion.2), channel_id=1, source_target_pairs={{0,2},{2,0},{1,3},{3,1},{4,6},{6,4},{5,7},{7,5},{8,10},{10,8},{9,1... | collective-permute-start | bytes 3145736 | tf_op jit(solution)/shard_map/ppermute | solution.py:24
  97.6 33.5 %collective-permute-start.10 = (bf16[2,256,2048]{2,1,0:T(8,128)(2,1)S(1)}, bf16[2,256,2048]{2,1,0:T(8,128)(2,1)S(1)}, u32[]{:S(2)}, u32[]{:S(2)}) collective-permute-start(bf16[2,256,2048]{2,1,0:T(8,128)(2,1)S(1)} %pad_maximum_fusion.1), channel_id=1, source_target_pairs={{0,1},{1,0},{2,3},{3,2},{4,5},{5,4},{6,7},{7,6},{8,9},{9,8},{10,11... | collective-permute-start | bytes 6291464 | tf_op jit(solution)/shard_map/ppermute | solution.py:24
  106.5 42.1 %copy-start.2 = (bf16[2,2,4,2,32,512]{5,4,3,2,1,0:T(8,128)(2,1)}, bf16[2,2,4,2,32,512]{5,4,3,2,1,0:T(8,128)(2,1)S(1)}, u32[]{:S(2)}) copy-start(bf16[2,2,4,2,32,512]{5,4,3,2,1,0:T(8,128)(2,1)S(1)} %get-tuple-element.20.refs_0_) | copy-start | bytes 3145732
  106.5 18.0 %collective-permute-start.13 = (bf16[2,2,4,2,32,512]{5,4,3,2,1,0:T(8,128)(2,1)S(1)}, bf16[2,2,4,2,32,512]{5,4,3,2,1,0:T(8,128)(2,1)S(1)}, u32[]{:S(2)}, u32[]{:S(2)}) collective-permute-start(bf16[2,2,4,2,32,512]{5,4,3,2,1,0:T(8,128)(2,1)S(1)} %get-tuple-element.20.refs_0_), channel_id=1, source_target_pairs={{192,0},{61,1},{196,4},{1,5},{200,8},{5,9},{204,12},{9,13},{208,16... | collective-permute-start | bytes 3145736 | tf_op jit(solution)/shard_map/ppermute | solution.py:38
  110.6 15.8 %collective-permute-start.12 = (bf16[2,2,4,2,32,512]{5,4,3,2,1,0:T(8,128)(2,1)S(1)}, bf16[2,2,4,2,32,512]{5,4,3,2,1,0:T(8,128)(2,1)S(1)}, u32[]{:S(2)}, u32[]{:S(2)}) collective-permute-start(bf16[2,2,4,2,32,512]{5,4,3,2,1,0:T(8,128)(2,1)S(1)} %get-tuple-element.19.refs_1_), channel_id=1, source_target_pairs={{64,0},{5,1},{68,4},{9,5},{72,8},{13,9},{76,12},{17,13},{80,16},{2... | collective-permute-start | bytes 3145736 | tf_op jit(solution)/shard_map/ppermute | solution.py:38
  114.1 49.7 %copy-start.16 = (s32[3]{0:T(128)}, s32[3]{0:T(128)S(1)}, u32[]{:S(2)}) copy-start(s32[3]{0:T(128)S(1)} %pad_add_fusion.place) | copy-start | bytes 40
  114.1 23.6 %collective-permute-start.11 = (bf16[2,2,4,2,32,512]{5,4,3,2,1,0:T(8,128)(2,1)S(1)}, bf16[2,2,4,2,32,512]{5,4,3,2,1,0:T(8,128)(2,1)S(1)}, u32[]{:S(2)}, u32[]{:S(2)}) collective-permute-start(bf16[2,2,4,2,32,512]{5,4,3,2,1,0:T(8,128)(2,1)S(1)} %get-tuple-element.20.refs_0_), channel_id=1, source_target_pairs={{64,0},{5,1},{68,4},{9,5},{72,8},{13,9},{76,12},{17,13},{80,16},{2... | collective-permute-start | bytes 3145736 | tf_op jit(solution)/shard_map/ppermute | solution.py:38
  117.5 20.3 %collective-permute-start.16 = (bf16[2,2,4,2,32,512]{5,4,3,2,1,0:T(8,128)(2,1)S(1)}, bf16[2,2,4,2,32,512]{5,4,3,2,1,0:T(8,128)(2,1)S(1)}, u32[]{:S(2)}, u32[]{:S(2)}) collective-permute-start(bf16[2,2,4,2,32,512]{5,4,3,2,1,0:T(8,128)(2,1)S(1)} %get-tuple-element.19.refs_1_), channel_id=1, source_target_pairs={{192,0},{61,1},{196,4},{1,5},{200,8},{5,9},{204,12},{9,13},{208,16... | collective-permute-start | bytes 3145736 | tf_op jit(solution)/shard_map/ppermute | solution.py:38
  124.6 24.1 %copy-start.4 = (bf16[2,2,4,2,32,512]{5,4,3,2,1,0:T(8,128)(2,1)}, bf16[2,2,4,2,32,512]{5,4,3,2,1,0:T(8,128)(2,1)S(1)}, u32[]{:S(2)}) copy-start(bf16[2,2,4,2,32,512]{5,4,3,2,1,0:T(8,128)(2,1)S(1)} %collective-permute-done.13.refs_6_) | copy-start | bytes 3145732
  124.6 22.2 %collective-permute-start.14 = (bf16[2,2,4,2,32,512]{5,4,3,2,1,0:T(8,128)(2,1)S(1)}, bf16[2,2,4,2,32,512]{5,4,3,2,1,0:T(8,128)(2,1)S(1)}, u32[]{:S(2)}, u32[]{:S(2)}) collective-permute-start(bf16[2,2,4,2,32,512]{5,4,3,2,1,0:T(8,128)(2,1)S(1)} %collective-permute-done.13.refs_6_), channel_id=1, source_target_pairs={{192,0},{61,1},{196,4},{1,5},{200,8},{5,9},{204,12},{9,13},{208,16... | collective-permute-start | bytes 3145736 | tf_op jit(solution)/shard_map/ppermute | solution.py:38
  126.5 22.2 %collective-permute-start.15 = (bf16[2,2,4,2,32,512]{5,4,3,2,1,0:T(8,128)(2,1)S(1)}, bf16[2,2,4,2,32,512]{5,4,3,2,1,0:T(8,128)(2,1)S(1)}, u32[]{:S(2)}, u32[]{:S(2)}) collective-permute-start(bf16[2,2,4,2,32,512]{5,4,3,2,1,0:T(8,128)(2,1)S(1)} %collective-permute-done.12.refs_3_), channel_id=1, source_target_pairs={{64,0},{5,1},{68,4},{9,5},{72,8},{13,9},{76,12},{17,13},{80,16},{2... | collective-permute-start | bytes 3145736 | tf_op jit(solution)/shard_map/ppermute | solution.py:38
  156.1 24.9 %collective-permute-start.17 = (bf16[3,512,512]{2,1,0:T(8,128)(2,1)}, bf16[3,512,512]{2,1,0:T(8,128)(2,1)}, u32[]{:S(2)}, u32[]{:S(2)}) collective-permute-start(bf16[3,512,512]{2,1,0:T(8,128)(2,1)} %given.1), channel_id=1, source_target_pairs={{0,1},{1,0},{2,3},{3,2},{4,5},{5,4},{6,7},{7,6},{8,9},{9,8},{10,11... | collective-permute-start | bytes 4718600 | tf_op jit(solution)/shard_map/ppermute | solution.py:24
  158.1 5.1 %collective-permute-start.18 = (bf16[16,1024]{1,0:T(8,128)(2,1)S(1)}, bf16[16,1024]{1,0:T(8,128)(2,1)S(1)}, u32[]{:S(2)}, u32[]{:S(2)}) collective-permute-start(bf16[16,1024]{1,0:T(8,128)(2,1)S(1)} %constant_dynamic-slice_fusion), channel_id=1, source_target_pairs={{0,4},{4,0},{8,12},{12,8},{1,5},{5,1},{9,13},{13,9},{2,6},{6,2},{1... | collective-permute-start | bytes 98312 | tf_op jit(solution)/shard_map/ppermute | solution.py:28
  (16 other events, 129.1 us)
where the time goes:
time: 232 us; the launch traced here: 230 us
  starting transfers between devices  80.6 us (35%)
  waiting for transfers between devices  64.6 us (28%)
  Pallas kernels  63.8 us (28%)
  local copies, waits for them, and re-layouts  12.3 us (5%)
  other arithmetic  7.85 us (3%)
    pallas_call x1, Pallas kernels, outputs(): pl.pallas_call(merge_kernel, out_shape=wide, in_specs=[SMEM, HBM, HBM, HB...  49.4 us
    ppermute x9, waiting for transfers between devices, along(): return lax.ppermute(array, PLANE, pairs)  33.6 us
    ppermute x9, starting transfers between devices, along(): return lax.ppermute(array, PLANE, pairs)  28 us
    ppermute x5, starting transfers between devices, swap(): return lax.ppermute(array, axis, [(0, 1), (1, 0)])  26.9 us
    ppermute x5, waiting for transfers between devices, swap(): return lax.ppermute(array, axis, [(0, 1), (1, 0)])  23.8 us
    ppermute x3, starting transfers between devices, near_weight(): lax.ppermute(piece, 'u', [((i + d) % NU, i) for i in range(NU)])  20 us
    unnamed x50, local copies, waits for them, and re-layouts  10.4 us
    pallas_call x1, Pallas kernels, outputs(): pl.pallas_call(given_kernel, out_shape=parts, in_specs=[SMEM, VMEM, VMEM]...  7.36 us
  transfers between devices with their start and end apart: 19, of which 11 were waited for; matrix products, arithmetic and copies ran while one was open for 3% of the time, Pallas kernels for 3%

commit v1 on v0

--- a/solution.py
+++ b/solution.py
@@ -44,29 +44,19 @@
     return jnp.concatenate([first, second], dim)
 
 
-def in_place(parts, me):
-    n = len(parts)
-    twice = jnp.stack(parts + parts[:-1])
-    return lax.dynamic_slice_in_dim(twice, (n - me) % n, n, 0)
-
-
 def near_weight(proj_old):
-    y, x, w, c = (lax.axis_index(a) for a in "yxwc")
+    c = lax.axis_index("c")
     half = proj_old.shape[1] // 2
     mine = lax.dynamic_slice_in_dim(proj_old, c * half, half, 1)
     given = lax.dynamic_slice_in_dim(proj_old, (1 - c) * half, half, 1)
-    piece = both(c, mine[None], swap(given, "c")[None], 0)
-    far = [piece] + [lax.ppermute(piece, "u", [((i + d) % NU, i) for i in range(NU)]) for d in (2, 1, 3)]
-    far[1], far[2] = far[2], far[1]
-    mates = in_place(far, lax.axis_index("u"))
-    other = swap(mates, "y")
-    planes = both(y, mates[None], other[None], 0)
-    near = [planes] + [along(planes, 1, d) for d in (1, 2, -1)]
-    return in_place(near, jnp.where(c == 0, w, x))
-
-
-def all_weight(slab):
-    low, high = slab[: slab.shape[0] // 2], slab[slab.shape[0] // 2 :]
+    taken = swap(given, "c")
+    mates = lax.all_gather(jnp.stack([mine, taken]), "u")
+    planes = lax.all_gather(mates, "y")
+    return [planes] + [along(planes, 1, d) for d in (1, 2, -1)]
+
+
+def all_weight(pieces):
+    low, high = lax.optimization_barrier((jnp.stack(pieces[:2]), jnp.stack(pieces[2:])))
     low_prev = along(low, 0, -1)
     high_next = along(high, 0, 1)
     high_prev = along(high, 0, -1)
@@ -119,8 +109,8 @@
             ref = slabs[2 * r + s]
             for t in range(2):
                 q = 2 * s + t
-                col = jnp.where(c == 0, lax.rem(x + r, 4), q)
-                row = jnp.where(c == 0, q, lax.rem(w + r, 4))
+                col = lax.rem(x + jnp.where(c == 0, r, q), NX)
+                row = lax.rem(w + jnp.where(c == 0, q, r), NW)
                 for y in range(2):
                     copies.append(
                         pltpu.make_async_copy(
@@ -148,7 +138,7 @@
     def store(block, i, values):
         out[block, i : i + ROWS, :] = values
 
-    products(place, 1 - place[2], vlm, action, slabs, weight, sems, store)
+    products(place, 1, vlm, action, slabs, weight, sems, store)
 
 
 def column_copies(core, parts, vlm_out, action_out, sems):
@@ -174,7 +164,7 @@
         if i + ROWS == stage.shape[1]:
             outs[block].start()
 
-    products(place, place[2], vlm, action, slabs, weight, sems, store)
+    products(place, 0, vlm, action, slabs, weight, sems, store)
     for copy in outs:
         copy.wait()
 
@@ -199,7 +189,7 @@
     cost = pl.CostEstimate(
         flops=6 * count * action.shape[1] * half, bytes_accessed=12 * 1024 * 1024, transcendentals=0
     )
-    params = pltpu.CompilerParams(vmem_limit_bytes=20 * 1024 * 1024)
+    params = pltpu.CompilerParams(vmem_limit_bytes=12 * 1024 * 1024)
     weight = pltpu.VMEM((2, 2, NX, NU, 2, rows, half), jnp.bfloat16)
     sems = pltpu.SemaphoreType.DMA((32,))
     parts = jax.ShapeDtypeStruct((3, count, half), jnp.bfloat16)
@@ -231,7 +221,7 @@
     return pl.pallas_call(
         merge_kernel,
         out_shape=wide,
-        in_specs=[SMEM, HBM, HBM, HBM],
+        in_specs=[SMEM, VMEM, HBM, HBM],
         out_specs=(HBM, HBM),
         scratch_shapes=[pltpu.SemaphoreType.DMA((3,))],
         input_output_aliases={2: 0, 3: 1},
@@ -240,12 +230,13 @@
 
 
 def local(vlm_tokens, action_tokens, norm_gain, proj_old):
-    slab, mine = near_weight(proj_old), chip_tokens(vlm_tokens, action_tokens, norm_gain)
-    slab, mine = lax.optimization_barrier((slab, mine))
-    slabs = all_weight(slab)
+    pieces = near_weight(proj_old)
+    mine = chip_tokens(vlm_tokens, action_tokens, norm_gain)
+    slabs = all_weight(pieces)
     vlm, action = all_tokens(mine, vlm_tokens.shape[0])
     vlm_hidden, action_hidden = outputs(vlm, action, slabs)
-    return (vlm_hidden, action_hidden, new_projection(proj_old))
+    new = new_projection(proj_old)
+    return (vlm_hidden, action_hidden, new)
 
 
 def solution(mesh):

time: 232 us -> 184 us (0.79)
  Pallas kernels: 63.8 us -> 18 us
  blocking collectives: 0 us -> 30.1 us
  waiting for transfers between devices: 64.6 us -> 48.7 us
  starting transfers between devices: 80.6 us -> 65.6 us
  local copies, waits for them, and re-layouts: 12.3 us -> 7.23 us
  other arithmetic: 7.85 us -> 12.4 us
    pallas_call x1, Pallas kernels: 49.4 us -> 2.59 us  [outputs(): pl.pallas_call(merge_kernel, out_shape=wide, in_specs=[SMEM, VMEM, HBM, H...]
    all_gather x0 -> x2, blocking collectives: none -> 30.1 us  [the longest x1 24.2 us: near_weight(): mates = lax.all_gather(jnp.stack([mine, taken]), 'u')]
    ppermute x3 -> x0, starting transfers between devices: 20 us -> none  [near_weight(): lax.ppermute(piece, 'u', [((i + d) % NU, i) for i in range(NU)])]
    ppermute x5 -> x4, waiting for transfers between devices: 23.8 us -> 17 us  [swap(): return lax.ppermute(array, axis, [(0, 1), (1, 0)])]
    ppermute x3 -> x0, waiting for transfers between devices: 5.91 us -> none  [near_weight(): lax.ppermute(piece, 'u', [((i + d) % NU, i) for i in range(NU)])]
    ppermute x9, waiting for transfers between devices: 33.6 us -> 27.8 us  [along(): return lax.ppermute(array, PLANE, pairs)]
    unnamed x50 -> x28, local copies, waits for them, and re-layouts: 10.4 us -> 6.53 us
    ppermute x5 -> x4, starting transfers between devices: 26.9 us -> 30.1 us  [swap(): return lax.ppermute(array, axis, [(0, 1), (1, 0)])]
  transfers between devices with their start and end apart: 19 -> 15, of which waited for: 11 -> 11; matrix products, arithmetic and copies ran while one was open for 3% -> 6% of each run, Pallas kernels for 3% -> 4%
where the time goes in v1:
time: 184 us; the launch traced here: 183 us
  starting transfers between devices  65.6 us (36%)
  waiting for transfers between devices  48.7 us (26%)
  blocking collectives  30.1 us (16%)
  Pallas kernels  18 us (10%)
  other arithmetic  12.4 us (7%)
  local copies, waits for them, and re-layouts  7.23 us (4%)
    ppermute x4, starting transfers between devices, swap(): return lax.ppermute(array, axis, [(0, 1), (1, 0)])  30.1 us
    ppermute x9, starting transfers between devices, along(): return lax.ppermute(array, PLANE, pairs)  29.2 us
    ppermute x9, waiting for transfers between devices, along(): return lax.ppermute(array, PLANE, pairs)  27.8 us
    all_gather x1, blocking collectives, near_weight(): mates = lax.all_gather(jnp.stack([mine, taken]), 'u')  24.2 us
    ppermute x4, waiting for transfers between devices, swap(): return lax.ppermute(array, axis, [(0, 1), (1, 0)])  17 us
    pallas_call x1, Pallas kernels, outputs(): pl.pallas_call(given_kernel, out_shape=parts, in_specs=[SMEM, VMEM, VMEM]...  7.89 us
    pallas_call x1, Pallas kernels, outputs(): pl.pallas_call(own_kernel, out_shape=wide, in_specs=[SMEM, VMEM, VMEM] +...  7.54 us
    unnamed x28, local copies, waits for them, and re-layouts  6.53 us
  transfers between devices with their start and end apart: 15, of which 11 were waited for; matrix products, arithmetic and copies ran while one was open for 6% of the time, Pallas kernels for 4%

profile of v1, /device:TPU:1, one launch (start us, length us, event | category | flops | bytes accessed | tf_op | source)
XLA Modules:
  0.0 183.1 jit_solution(1844286057172547119)
XLA Ops:
  2.9 4.4 %collective-permute-start = (bf16[64,2048]{1,0:T(8,128)(2,1)S(1)}, bf16[64,2048]{1,0:T(8,128)(2,1)S(1)}, u32[]{:S(2)}, u32[]{:S(2)}) collective-permute-start(bf16[64,2048]{1,0:T(8,128)(2,1)S(1)} %fusion.5), channel_id=1, source_target_pairs={{0,4},{4,0},{8,12},{12,8},{1,5},{5,1},{9,13},{13,9},{2,6},{6,2},{1... | collective-permute-start | bytes 786440 | tf_op jit(solution)/shard_map/ppermute | solution.py:28
  11.4 7.0 %collective-permute-start.1 = (bf16[256,2048]{1,0:T(8,128)(2,1)S(1)}, bf16[256,2048]{1,0:T(8,128)(2,1)}, u32[]{:S(2)}, u32[]{:S(2)}) collective-permute-start(bf16[256,2048]{1,0:T(8,128)(2,1)S(1)} %pad_maximum_fusion.2), channel_id=1, source_target_pairs={{0,2},{2,0},{1,3},{3,1},{4,6},{6,4},{5,7},{7,5},{8,10},{10,8},{9,1... | collective-permute-start | bytes 3145736 | tf_op jit(solution)/shard_map/ppermute | solution.py:24
  18.4 3.8 %collective-permute-start.3 = (bf16[32,512]{1,0:T(8,128)(2,1)S(1)}, bf16[32,512]{1,0:T(8,128)(2,1)S(1)}, u32[]{:S(2)}, u32[]{:S(2)}) collective-permute-start(bf16[32,512]{1,0:T(8,128)(2,1)S(1)} %get-tuple-element.26), channel_id=1, source_target_pairs={{0,1},{1,0},{2,3},{3,2},{4,5},{5,4},{6,7},{7,6},{8,9},{9,8},{10,11... | collective-permute-start | bytes 98312 | tf_op jit(solution)/shard_map/ppermute | solution.py:24
  22.2 16.9 %collective-permute-done.1 = bf16[256,2048]{1,0:T(8,128)(2,1)} collective-permute-done((bf16[256,2048]{1,0:T(8,128)(2,1)S(1)}, bf16[256,2048]{1,0:T(8,128)(2,1)}, u32[]{:S(2)}, u32[]{:S(2)}) %collective-permute-start.1) | collective-permute-done | bytes 1048608 | tf_op jit(solution)/shard_map/ppermute | solution.py:24
  42.4 5.3 %collective-permute-start.2 = (bf16[2,256,2048]{2,1,0:T(8,128)(2,1)}, bf16[2,256,2048]{2,1,0:T(8,128)(2,1)}, u32[]{:S(2)}, u32[]{:S(2)}) collective-permute-start(bf16[2,256,2048]{2,1,0:T(8,128)(2,1)} %pad_maximum_fusion.1), channel_id=1, source_target_pairs={{0,1},{1,0},{2,3},{3,2},{4,5},{5,4},{6,7},{7,6},{8,9},{9,8},{10,11... | collective-permute-start | bytes 6291464 | tf_op jit(solution)/shard_map/ppermute | solution.py:24
  47.7 24.2 %all-gather = bf16[8,32,512]{2,1,0:T(8,128)(2,1)S(1)} all-gather(bf16[2,32,512]{2,1,0:T(8,128)(2,1)S(1)} %pad_maximum_fusion.5), channel_id=2, replica_groups=mesh['y'=2,'x'=4,'u'=4,'w'=4,'h'=2,'c'=2] {'u'}, dimensions={0}, use_global_device_ids=true | all-gather | bytes 327680 | tf_op jit(solution)/shard_map/all_gather | solution.py:53
  71.9 5.9 %all-gather.1 = bf16[8,2,32,512]{3,2,1,0:T(8,128)(2,1)S(1)} all-gather(bf16[4,2,32,512]{3,2,1,0:T(8,128)(2,1)S(1)} %bitcast.38), channel_id=3, replica_groups=mesh['y'=2,'x'=4,'u'=4,'w'=4,'h'=2,'c'=2] {'y'}, dimensions={0}, use_global_device_ids=true | all-gather | bytes 786432 | tf_op jit(solution)/shard_map/all_gather | solution.py:54
  77.8 4.6 %collective-permute-start.5 = (bf16[2,4,2,32,512]{4,3,2,1,0:T(8,128)(2,1)S(1)}, bf16[2,4,2,32,512]{4,3,2,1,0:T(8,128)(2,1)S(1)}, u32[]{:S(2)}, u32[]{:S(2)}) collective-permute-start(bf16[2,4,2,32,512]{4,3,2,1,0:T(8,128)(2,1)S(1)} %bitcast.34), channel_id=1, source_target_pairs={{8,0},{129,1},{12,4},{133,5},{16,8},{137,9},{20,12},{141,13},{24,1... | collective-permute-start | bytes 1572872 | tf_op jit(solution)/shard_map/ppermute | solution.py:38
  82.4 2.2 %collective-permute-start.6 = (bf16[2,4,2,32,512]{4,3,2,1,0:T(8,128)(2,1)S(1)}, bf16[2,4,2,32,512]{4,3,2,1,0:T(8,128)(2,1)S(1)}, u32[]{:S(2)}, u32[]{:S(2)}) collective-permute-start(bf16[2,4,2,32,512]{4,3,2,1,0:T(8,128)(2,1)S(1)} %bitcast.35), channel_id=1, source_target_pairs={{60,0},{193,1},{0,4},{197,5},{4,8},{201,9},{8,12},{205,13},{12,16}... | collective-permute-start | bytes 1572872 | tf_op jit(solution)/shard_map/ppermute | solution.py:38
  84.7 4.3 %collective-permute-start.4 = (bf16[2,4,2,32,512]{4,3,2,1,0:T(8,128)(2,1)S(1)}, bf16[2,4,2,32,512]{4,3,2,1,0:T(8,128)(2,1)S(1)}, u32[]{:S(2)}, u32[]{:S(2)}) collective-permute-start(bf16[2,4,2,32,512]{4,3,2,1,0:T(8,128)(2,1)S(1)} %bitcast.36), channel_id=1, source_target_pairs={{4,0},{65,1},{8,4},{69,5},{12,8},{73,9},{16,12},{77,13},{20,16},{8... | collective-permute-start | bytes 1572872 | tf_op jit(solution)/shard_map/ppermute | solution.py:38
  89.3 5.8 %collective-permute-done.6 = bf16[2,4,2,32,512]{4,3,2,1,0:T(8,128)(2,1)S(1)} collective-permute-done((bf16[2,4,2,32,512]{4,3,2,1,0:T(8,128)(2,1)S(1)}, bf16[2,4,2,32,512]{4,3,2,1,0:T(8,128)(2,1)S(1)}, u32[]{:S(2)}, u32[]{:S(2)}) %collective-permute-start.6) | collective-permute-done | bytes 524320 | tf_op jit(solution)/shard_map/ppermute | solution.py:38
  96.3 2.5 %collective-permute-start.9 = (bf16[2,2,4,2,32,512]{5,4,3,2,1,0:T(8,128)(2,1)}, bf16[2,2,4,2,32,512]{5,4,3,2,1,0:T(8,128)(2,1)}, u32[]{:S(2)}, u32[]{:S(2)}) collective-permute-start(bf16[2,2,4,2,32,512]{5,4,3,2,1,0:T(8,128)(2,1)} %pad_maximum_fusion.3.refs_0_), channel_id=1, source_target_pairs={{192,0},{61,1},{196,4},{1,5},{200,8},{5,9},{204,12},{9,13},{208,16... | collective-permute-start | bytes 3145736 | tf_op jit(solution)/shard_map/ppermute | solution.py:38
  98.8 4.0 %collective-permute-start.8 = (bf16[2,2,4,2,32,512]{5,4,3,2,1,0:T(8,128)(2,1)S(1)}, bf16[2,2,4,2,32,512]{5,4,3,2,1,0:T(8,128)(2,1)}, u32[]{:S(2)}, u32[]{:S(2)}) collective-permute-start(bf16[2,2,4,2,32,512]{5,4,3,2,1,0:T(8,128)(2,1)S(1)} %pad_maximum_fusion.4.refs_1_), channel_id=1, source_target_pairs={{64,0},{5,1},{68,4},{9,5},{72,8},{13,9},{76,12},{17,13},{80,16},{2... | collective-permute-start | bytes 3145736 | tf_op jit(solution)/shard_map/ppermute | solution.py:38
  104.8 4.6 %collective-permute-start.7 = (bf16[2,2,4,2,32,512]{5,4,3,2,1,0:T(8,128)(2,1)}, bf16[2,2,4,2,32,512]{5,4,3,2,1,0:T(8,128)(2,1)S(1)}, u32[]{:S(2)}, u32[]{:S(2)}) collective-permute-start(bf16[2,2,4,2,32,512]{5,4,3,2,1,0:T(8,128)(2,1)} %pad_maximum_fusion.3.refs_0_), channel_id=1, source_target_pairs={{64,0},{5,1},{68,4},{9,5},{72,8},{13,9},{76,12},{17,13},{80,16},{2... | collective-permute-start | bytes 3145736 | tf_op jit(solution)/shard_map/ppermute | solution.py:38
  109.4 4.0 %collective-permute-done.9.refs_6_ = bf16[2,2,4,2,32,512]{5,4,3,2,1,0:T(8,128)(2,1)} collective-permute-done((bf16[2,2,4,2,32,512]{5,4,3,2,1,0:T(8,128)(2,1)}, bf16[2,2,4,2,32,512]{5,4,3,2,1,0:T(8,128)(2,1)}, u32[]{:S(2)}, u32[]{:S(2)}) %collective-permute-start.9) | collective-permute-done | bytes 1048608 | tf_op jit(solution)/shard_map/ppermute | solution.py:38
  116.7 3.2 %collective-permute-start.11 = (bf16[2,2,4,2,32,512]{5,4,3,2,1,0:T(8,128)(2,1)}, bf16[2,2,4,2,32,512]{5,4,3,2,1,0:T(8,128)(2,1)S(1)}, u32[]{:S(2)}, u32[]{:S(2)}) collective-permute-start(bf16[2,2,4,2,32,512]{5,4,3,2,1,0:T(8,128)(2,1)} %collective-permute-done.8.refs_3_), channel_id=1, source_target_pairs={{64,0},{5,1},{68,4},{9,5},{72,8},{13,9},{76,12},{17,13},{80,16},{2... | collective-permute-start | bytes 3145736 | tf_op jit(solution)/shard_map/ppermute | solution.py:38
  124.9 3.1 %collective-permute-done.7.refs_2_ = bf16[2,2,4,2,32,512]{5,4,3,2,1,0:T(8,128)(2,1)S(1)} collective-permute-done((bf16[2,2,4,2,32,512]{5,4,3,2,1,0:T(8,128)(2,1)}, bf16[2,2,4,2,32,512]{5,4,3,2,1,0:T(8,128)(2,1)S(1)}, u32[]{:S(2)}, u32[]{:S(2)}) %collective-permute-start.7) | collective-permute-done | bytes 1048608 | tf_op jit(solution)/shard_map/ppermute | solution.py:38
  128.0 8.0 %collective-permute-done.10.refs_4_ = bf16[2,2,4,2,32,512]{5,4,3,2,1,0:T(8,128)(2,1)S(1)} collective-permute-done((bf16[2,2,4,2,32,512]{5,4,3,2,1,0:T(8,128)(2,1)}, bf16[2,2,4,2,32,512]{5,4,3,2,1,0:T(8,128)(2,1)S(1)}, u32[]{:S(2)}, u32[]{:S(2)}) %collective-permute-start.10) | collective-permute-done | bytes 1048608 | tf_op jit(solution)/shard_map/ppermute | solution.py:38
  136.0 3.1 %collective-permute-done.11.refs_5_ = bf16[2,2,4,2,32,512]{5,4,3,2,1,0:T(8,128)(2,1)S(1)} collective-permute-done((bf16[2,2,4,2,32,512]{5,4,3,2,1,0:T(8,128)(2,1)}, bf16[2,2,4,2,32,512]{5,4,3,2,1,0:T(8,128)(2,1)S(1)}, u32[]{:S(2)}, u32[]{:S(2)}) %collective-permute-start.11) | collective-permute-done | bytes 1048608 | tf_op jit(solution)/shard_map/ppermute | solution.py:38
  139.1 7.9 %given.1 = bf16[3,512,512]{2,1,0:T(8,128)(2,1)} custom-call(s32[3]{0:T(128)S(1)} %pad_add_fusion.place, bf16[512,2048]{1,0:T(8,128)(2,1)S(1)} %bitcast.28, bf16[512,2048]{1,0:T(8,128)(2,1)S(1)} %bitcast.30, bf16[2,2,4,2,32,512]{5,4,3,2,1,0:T(8,128)(2,1)} %pad_maximum_fusion.3.refs_0_, bf16[2,2,4,2,32,512]{5,4,3,2,1,0:T(8,128)(2,1)S(1)} %pad_maximum_fusion.4.refs_1_, ...), custom_call_target="tpu_custom_call" | custom-call | flops 3221225472 | bytes 12582912 | tf_op jit(solution)/shard_map/given/pallas_call | solution.py:200
  147.0 14.1 %collective-permute-start.13 = (bf16[3,512,512]{2,1,0:T(8,128)(2,1)}, bf16[3,512,512]{2,1,0:T(8,128)(2,1)}, u32[]{:S(2)}, u32[]{:S(2)}) collective-permute-start(bf16[3,512,512]{2,1,0:T(8,128)(2,1)} %given.1), channel_id=1, source_target_pairs={{0,1},{1,0},{2,3},{3,2},{4,5},{5,4},{6,7},{7,6},{8,9},{9,8},{10,11... | collective-permute-start | bytes 4718600 | tf_op jit(solution)/shard_map/ppermute | solution.py:24
  163.0 2.7 %collective-permute-done.14 = bf16[16,1024]{1,0:T(8,128)(2,1)S(1)} collective-permute-done((bf16[16,1024]{1,0:T(8,128)(2,1)S(1)}, bf16[16,1024]{1,0:T(8,128)(2,1)S(1)}, u32[]{:S(2)}, u32[]{:S(2)}) %collective-permute-start.14) | collective-permute-done | bytes 32800 | tf_op jit(solution)/shard_map/ppermute | solution.py:28
  172.9 7.5 %own.1 = (bf16[512,1024]{1,0:T(8,128)(2,1)}, bf16[512,2048]{1,0:T(8,128)(2,1)}) custom-call(s32[3]{0:T(128)S(1)} %pad_add_fusion.place, bf16[512,2048]{1,0:T(8,128)(2,1)S(1)} %bitcast.29, bf16[512,2048]{1,0:T(8,128)(2,1)S(1)} %bitcast.31, bf16[2,2,4,2,32,512]{5,4,3,2,1,0:T(8,128)(2,1)} %pad_maximum_fusion.3.refs_0_, ...), custom_call_target="tpu_custom_call" | custom-call | flops 3221225472 | bytes 12582912 | tf_op jit(solution)/shard_map/own/pallas_call | solution.py:210
  180.5 2.6 %merge.1 = (bf16[512,1024]{1,0:T(8,128)(2,1)}, bf16[512,2048]{1,0:T(8,128)(2,1)}) custom-call(s32[3]{0:T(128)} %copy-done.10, bf16[3,512,512]{2,1,0:T(8,128)(2,1)} %collective-permute-done.13.parts, bf16[512,1024]{1,0:T(8,128)(2,1)} %get-tuple-element.11.vlm_in, ...), custom_call_target="tpu_custom_call", output_to_operand_aliasing={{0}: (2, {}), {1}: (3, {})} | custom-call | tf_op jit(solution)/shard_map/merge/pallas_call | solution.py:221
  (61 shorter events, 30.4 us)
Async XLA Ops:
  0.6 10.4 %copy-start.11 = (bf16[64,2048]{1,0:T(8,128)(2,1)S(1)}, bf16[64,2048]{1,0:T(8,128)(2,1)}, u32[]{:S(2)}) copy-start(bf16[64,2048]{1,0:T(8,128)(2,1)} %param.4) | copy-start | bytes 786436
  0.6 10.4 %copy-start.13 = (f32[2048]{0:T(1024)S(1)}, f32[2048]{0:T(1024)}, u32[]{:S(2)}) copy-start(f32[2048]{0:T(1024)} %param.6) | copy-start | bytes 24580
  2.9 8.1 %collective-permute-start = (bf16[64,2048]{1,0:T(8,128)(2,1)S(1)}, bf16[64,2048]{1,0:T(8,128)(2,1)S(1)}, u32[]{:S(2)}, u32[]{:S(2)}) collective-permute-start(bf16[64,2048]{1,0:T(8,128)(2,1)S(1)} %fusion.5), channel_id=1, source_target_pairs={{0,4},{4,0},{8,12},{12,8},{1,5},{5,1},{9,13},{13,9},{2,6},{6,2},{1... | collective-permute-start | bytes 786440 | tf_op jit(solution)/shard_map/ppermute | solution.py:28
  8.5 9.8 %copy-start.12 = (bf16[32,1024]{1,0:T(8,128)(2,1)S(1)}, bf16[32,1024]{1,0:T(8,128)(2,1)}, u32[]{:S(2)}) copy-start(bf16[32,1024]{1,0:T(8,128)(2,1)} %param.7) | copy-start | bytes 196612
  11.4 27.8 %collective-permute-start.1 = (bf16[256,2048]{1,0:T(8,128)(2,1)S(1)}, bf16[256,2048]{1,0:T(8,128)(2,1)}, u32[]{:S(2)}, u32[]{:S(2)}) collective-permute-start(bf16[256,2048]{1,0:T(8,128)(2,1)S(1)} %pad_maximum_fusion.2), channel_id=1, source_target_pairs={{0,2},{2,0},{1,3},{3,1},{4,6},{6,4},{5,7},{7,5},{8,10},{10,8},{9,1... | collective-permute-start | bytes 3145736 | tf_op jit(solution)/shard_map/ppermute | solution.py:24
  18.4 29.3 %collective-permute-start.3 = (bf16[32,512]{1,0:T(8,128)(2,1)S(1)}, bf16[32,512]{1,0:T(8,128)(2,1)S(1)}, u32[]{:S(2)}, u32[]{:S(2)}) collective-permute-start(bf16[32,512]{1,0:T(8,128)(2,1)S(1)} %get-tuple-element.26), channel_id=1, source_target_pairs={{0,1},{1,0},{2,3},{3,2},{4,5},{5,4},{6,7},{7,6},{8,9},{9,8},{10,11... | collective-permute-start | bytes 98312 | tf_op jit(solution)/shard_map/ppermute | solution.py:24
  42.4 77.5 %collective-permute-start.2 = (bf16[2,256,2048]{2,1,0:T(8,128)(2,1)}, bf16[2,256,2048]{2,1,0:T(8,128)(2,1)}, u32[]{:S(2)}, u32[]{:S(2)}) collective-permute-start(bf16[2,256,2048]{2,1,0:T(8,128)(2,1)} %pad_maximum_fusion.1), channel_id=1, source_target_pairs={{0,1},{1,0},{2,3},{3,2},{4,5},{5,4},{6,7},{7,6},{8,9},{9,8},{10,11... | collective-permute-start | bytes 6291464 | tf_op jit(solution)/shard_map/ppermute | solution.py:24
  77.8 11.5 %collective-permute-start.5 = (bf16[2,4,2,32,512]{4,3,2,1,0:T(8,128)(2,1)S(1)}, bf16[2,4,2,32,512]{4,3,2,1,0:T(8,128)(2,1)S(1)}, u32[]{:S(2)}, u32[]{:S(2)}) collective-permute-start(bf16[2,4,2,32,512]{4,3,2,1,0:T(8,128)(2,1)S(1)} %bitcast.34), channel_id=1, source_target_pairs={{8,0},{129,1},{12,4},{133,5},{16,8},{137,9},{20,12},{141,13},{24,1... | collective-permute-start | bytes 1572872 | tf_op jit(solution)/shard_map/ppermute | solution.py:38
  82.4 12.7 %collective-permute-start.6 = (bf16[2,4,2,32,512]{4,3,2,1,0:T(8,128)(2,1)S(1)}, bf16[2,4,2,32,512]{4,3,2,1,0:T(8,128)(2,1)S(1)}, u32[]{:S(2)}, u32[]{:S(2)}) collective-permute-start(bf16[2,4,2,32,512]{4,3,2,1,0:T(8,128)(2,1)S(1)} %bitcast.35), channel_id=1, source_target_pairs={{60,0},{193,1},{0,4},{197,5},{4,8},{201,9},{8,12},{205,13},{12,16}... | collective-permute-start | bytes 1572872 | tf_op jit(solution)/shard_map/ppermute | solution.py:38
  84.7 10.6 %collective-permute-start.4 = (bf16[2,4,2,32,512]{4,3,2,1,0:T(8,128)(2,1)S(1)}, bf16[2,4,2,32,512]{4,3,2,1,0:T(8,128)(2,1)S(1)}, u32[]{:S(2)}, u32[]{:S(2)}) collective-permute-start(bf16[2,4,2,32,512]{4,3,2,1,0:T(8,128)(2,1)S(1)} %bitcast.36), channel_id=1, source_target_pairs={{4,0},{65,1},{8,4},{69,5},{12,8},{73,9},{16,12},{77,13},{20,16},{8... | collective-permute-start | bytes 1572872 | tf_op jit(solution)/shard_map/ppermute | solution.py:38
  96.3 17.1 %collective-permute-start.9 = (bf16[2,2,4,2,32,512]{5,4,3,2,1,0:T(8,128)(2,1)}, bf16[2,2,4,2,32,512]{5,4,3,2,1,0:T(8,128)(2,1)}, u32[]{:S(2)}, u32[]{:S(2)}) collective-permute-start(bf16[2,2,4,2,32,512]{5,4,3,2,1,0:T(8,128)(2,1)} %pad_maximum_fusion.3.refs_0_), channel_id=1, source_target_pairs={{192,0},{61,1},{196,4},{1,5},{200,8},{5,9},{204,12},{9,13},{208,16... | collective-permute-start | bytes 3145736 | tf_op jit(solution)/shard_map/ppermute | solution.py:38
  98.8 17.9 %collective-permute-start.8 = (bf16[2,2,4,2,32,512]{5,4,3,2,1,0:T(8,128)(2,1)S(1)}, bf16[2,2,4,2,32,512]{5,4,3,2,1,0:T(8,128)(2,1)}, u32[]{:S(2)}, u32[]{:S(2)}) collective-permute-start(bf16[2,2,4,2,32,512]{5,4,3,2,1,0:T(8,128)(2,1)S(1)} %pad_maximum_fusion.4.refs_1_), channel_id=1, source_target_pairs={{64,0},{5,1},{68,4},{9,5},{72,8},{13,9},{76,12},{17,13},{80,16},{2... | collective-permute-start | bytes 3145736 | tf_op jit(solution)/shard_map/ppermute | solution.py:38
  102.9 63.6 %copy-start.10 = (s32[3]{0:T(128)}, s32[3]{0:T(128)S(1)}, u32[]{:S(2)}) copy-start(s32[3]{0:T(128)S(1)} %pad_add_fusion.place) | copy-start | bytes 40
  102.9 22.0 %collective-permute-start.12 = (bf16[2,2,4,2,32,512]{5,4,3,2,1,0:T(8,128)(2,1)S(1)}, bf16[2,2,4,2,32,512]{5,4,3,2,1,0:T(8,128)(2,1)S(1)}, u32[]{:S(2)}, u32[]{:S(2)}) collective-permute-start(bf16[2,2,4,2,32,512]{5,4,3,2,1,0:T(8,128)(2,1)S(1)} %pad_maximum_fusion.4.refs_1_), channel_id=1, source_target_pairs={{192,0},{61,1},{196,4},{1,5},{200,8},{5,9},{204,12},{9,13},{208,16... | collective-permute-start | bytes 3145736 | tf_op jit(solution)/shard_map/ppermute | solution.py:38
  104.8 23.2 %collective-permute-start.7 = (bf16[2,2,4,2,32,512]{5,4,3,2,1,0:T(8,128)(2,1)}, bf16[2,2,4,2,32,512]{5,4,3,2,1,0:T(8,128)(2,1)S(1)}, u32[]{:S(2)}, u32[]{:S(2)}) collective-permute-start(bf16[2,2,4,2,32,512]{5,4,3,2,1,0:T(8,128)(2,1)} %pad_maximum_fusion.3.refs_0_), channel_id=1, source_target_pairs={{64,0},{5,1},{68,4},{9,5},{72,8},{13,9},{76,12},{17,13},{80,16},{2... | collective-permute-start | bytes 3145736 | tf_op jit(solution)/shard_map/ppermute | solution.py:38
  113.3 22.7 %collective-permute-start.10 = (bf16[2,2,4,2,32,512]{5,4,3,2,1,0:T(8,128)(2,1)}, bf16[2,2,4,2,32,512]{5,4,3,2,1,0:T(8,128)(2,1)S(1)}, u32[]{:S(2)}, u32[]{:S(2)}) collective-permute-start(bf16[2,2,4,2,32,512]{5,4,3,2,1,0:T(8,128)(2,1)} %collective-permute-done.9.refs_6_), channel_id=1, source_target_pairs={{192,0},{61,1},{196,4},{1,5},{200,8},{5,9},{204,12},{9,13},{208,16... | collective-permute-start | bytes 3145736 | tf_op jit(solution)/shard_map/ppermute | solution.py:38
  116.7 22.4 %collective-permute-start.11 = (bf16[2,2,4,2,32,512]{5,4,3,2,1,0:T(8,128)(2,1)}, bf16[2,2,4,2,32,512]{5,4,3,2,1,0:T(8,128)(2,1)S(1)}, u32[]{:S(2)}, u32[]{:S(2)}) collective-permute-start(bf16[2,2,4,2,32,512]{5,4,3,2,1,0:T(8,128)(2,1)} %collective-permute-done.8.refs_3_), channel_id=1, source_target_pairs={{64,0},{5,1},{68,4},{9,5},{72,8},{13,9},{76,12},{17,13},{80,16},{2... | collective-permute-start | bytes 3145736 | tf_op jit(solution)/shard_map/ppermute | solution.py:38
  122.7 16.3 %copy-start = (bf16[4,128,2048]{2,1,0:T(8,128)(2,1)}, bf16[4,128,2048]{2,1,0:T(8,128)(2,1)S(1)}, u32[]{:S(2)}) copy-start(bf16[4,128,2048]{2,1,0:T(8,128)(2,1)S(1)} %get-tuple-element.15) | copy-start | bytes 6291460
  124.9 22.1 %copy-start.2 = (bf16[2,2,4,2,32,512]{5,4,3,2,1,0:T(8,128)(2,1)}, bf16[2,2,4,2,32,512]{5,4,3,2,1,0:T(8,128)(2,1)S(1)}, u32[]{:S(2)}) copy-start(bf16[2,2,4,2,32,512]{5,4,3,2,1,0:T(8,128)(2,1)S(1)} %collective-permute-done.12.refs_7_) | copy-start | bytes 3145732
  127.9 19.0 %copy-start.4 = (bf16[2,2,4,2,32,512]{5,4,3,2,1,0:T(8,128)(2,1)}, bf16[2,2,4,2,32,512]{5,4,3,2,1,0:T(8,128)(2,1)S(1)}, u32[]{:S(2)}) copy-start(bf16[2,2,4,2,32,512]{5,4,3,2,1,0:T(8,128)(2,1)S(1)} %collective-permute-done.7.refs_2_) | copy-start | bytes 3145732
  136.0 11.0 %copy-start.6 = (bf16[2,2,4,2,32,512]{5,4,3,2,1,0:T(8,128)(2,1)}, bf16[2,2,4,2,32,512]{5,4,3,2,1,0:T(8,128)(2,1)S(1)}, u32[]{:S(2)}) copy-start(bf16[2,2,4,2,32,512]{5,4,3,2,1,0:T(8,128)(2,1)S(1)} %collective-permute-done.10.refs_4_) | copy-start | bytes 3145732
  139.1 7.9 %copy-start.8 = (bf16[2,2,4,2,32,512]{5,4,3,2,1,0:T(8,128)(2,1)}, bf16[2,2,4,2,32,512]{5,4,3,2,1,0:T(8,128)(2,1)S(1)}, u32[]{:S(2)}) copy-start(bf16[2,2,4,2,32,512]{5,4,3,2,1,0:T(8,128)(2,1)S(1)} %collective-permute-done.11.refs_5_) | copy-start | bytes 3145732
  147.0 33.4 %collective-permute-start.13 = (bf16[3,512,512]{2,1,0:T(8,128)(2,1)}, bf16[3,512,512]{2,1,0:T(8,128)(2,1)}, u32[]{:S(2)}, u32[]{:S(2)}) collective-permute-start(bf16[3,512,512]{2,1,0:T(8,128)(2,1)} %given.1), channel_id=1, source_target_pairs={{0,1},{1,0},{2,3},{3,2},{4,5},{5,4},{6,7},{7,6},{8,9},{9,8},{10,11... | collective-permute-start | bytes 4718600 | tf_op jit(solution)/shard_map/ppermute | solution.py:24
  161.1 4.7 %collective-permute-start.14 = (bf16[16,1024]{1,0:T(8,128)(2,1)S(1)}, bf16[16,1024]{1,0:T(8,128)(2,1)S(1)}, u32[]{:S(2)}, u32[]{:S(2)}) collective-permute-start(bf16[16,1024]{1,0:T(8,128)(2,1)S(1)} %constant_dynamic-slice_fusion), channel_id=1, source_target_pairs={{0,4},{4,0},{8,12},{12,8},{1,5},{5,1},{9,13},{13,9},{2,6},{6,2},{1... | collective-permute-start | bytes 98312 | tf_op jit(solution)/shard_map/ppermute | solution.py:28
  (5 other events, 6.5 us)
